TPU v7x, 32 devices: a whole 2x2x4 slice. The times are simulated.
32 devices in a mesh: row: 8 (over z, core), col: 4 (over y, x).
Axes of the slice: x: 2, y: 2, z: 4, core: 2. Of those that a mesh axis runs over, the one named last changes fastest.
Arguments:
- energy: float32 [4, 2048, 2048], P('col', 'row'), may hold values from 0.5 to 8
- damage_old: float32 [4, 2048, 2048], P('col', 'row'), may hold values from 0 to 0.8
- crack_seeds: int32 [4, 2048, 2048], P('col', 'row'), may hold values 0 or 1
- irreversible: int32 [4, 2048, 2048], P('col', 'row'), may hold values 0 or 1
- line_inverses: float32 [8, 256, 256], replicated, may hold values from -0.6 to 2.8
- z_inverse: float32 [4, 4], replicated, may hold values from -0.8 to 1.9
Outputs:
- damage: float32 [4, 2048, 2048], P('col', 'row')
- update_norms: float32 [2], replicated
All inputs are finite; a program needn't handle non-finite values. No bound on the sum of `crack_seeds` or of `irreversible` on one device may be relied on, other than what follows from the above.
Results may differ from a plain program's by a relative error of at most 0.0001.
Values sent between devices are 32-bit elements; how exact they have to be, the bound alone decides.
A program may use at most 128 MiB of HBM per device.

v0:
```python
import jax
import jax.numpy as jnp
from jax import lax
from jax.sharding import PartitionSpec as P

ITERS = 2
KAPPA = 2.0
STEP = 0.02
COUPLE = 0.5
EPSILON = 1e-06


def second_difference(grid_field, along):
    extent = grid_field.shape[along]
    forward_diff = lax.slice_in_dim(grid_field, 1, extent, axis=along) - lax.slice_in_dim(
        grid_field, 0, extent - 1, axis=along
    )
    zero_shape = list(grid_field.shape)
    zero_shape[along] = 1
    zero_rim = jnp.zeros(zero_shape, grid_field.dtype)
    ahead = jnp.concatenate([forward_diff, zero_rim], axis=along)
    behind = jnp.concatenate([zero_rim, forward_diff], axis=along)
    return ahead - behind


def line_solve(line_rows, inverses):
    block_count, block_cells, _ = inverses.shape
    line_count = line_rows.shape[0]
    blocks = line_rows.reshape(line_count, block_count, block_cells)
    products = jnp.einsum("rkb,kcb->rkc", blocks, inverses, precision=lax.Precision.HIGHEST)
    first_col = inverses[:, :, 0]
    last_col = inverses[:, :, block_cells - 1]
    incoming = [jnp.zeros((line_count,), line_rows.dtype)]
    for block_index in range(block_count - 1):
        incoming.append(
            products[:, block_index, block_cells - 1]
            + COUPLE * incoming[block_index] * inverses[block_index, block_cells - 1, 0]
        )
    inflow = jnp.stack(incoming, axis=1)
    forward = products + COUPLE * inflow[:, :, None] * first_col[None]
    head_terms = [jnp.zeros((line_count,), line_rows.dtype) for block_index in range(block_count)]
    carried = forward[:, block_count - 1, 0]
    for block_index in range(block_count - 2, -1, -1):
        head_terms[block_index] = carried
        carried = (
            forward[:, block_index, 0]
            + COUPLE * carried * inverses[block_index, 0, block_cells - 1]
        )
    outflow = jnp.stack(head_terms, axis=1)
    solved = forward + COUPLE * outflow[:, :, None] * last_col[None]
    return solved.reshape(line_count, block_count * block_cells)


def local(energy, damage_old, crack_seeds, irreversible, line_inverses, z_inverse):
    planes, rows_here, line_length = energy.shape
    row_count = lax.axis_size("row")
    col_count = lax.axis_size("col")
    total_planes = planes * col_count
    cell_count = total_planes * rows_here * row_count * line_length
    seeded = crack_seeds == 1
    damage = jnp.where(seeded, 1.0, damage_old)
    lower_bound = jnp.where(irreversible == 1, damage_old, 0.0)
    own_sums = []
    for sweep_index in range(ITERS):
        local_lap = second_difference(damage, 2)
        partial_value = energy - (1.0 + energy) * damage + KAPPA * local_lap
        moved_part, moved_damage = (
            lax.all_to_all(
                lax.all_to_all(
                    jnp.swapaxes(partial_value, 1, 2),
                    "row",
                    split_axis=1,
                    concat_axis=2,
                    tiled=True,
                ),
                "col",
                split_axis=1,
                concat_axis=0,
                tiled=True,
            ),
            lax.all_to_all(
                lax.all_to_all(
                    jnp.swapaxes(damage, 1, 2), "row", split_axis=1, concat_axis=2, tiled=True
                ),
                "col",
                split_axis=1,
                concat_axis=0,
                tiled=True,
            ),
        )
        lap_rest = second_difference(moved_damage, 2) + second_difference(moved_damage, 0)
        turned = moved_part + KAPPA * lap_rest
        turned_shape = turned.shape
        along_y = line_solve(turned.reshape(-1, turned_shape[2]), line_inverses).reshape(
            turned_shape
        )
        along_z = jnp.einsum("zk,kxy->zxy", z_inverse, along_y, precision=lax.Precision.HIGHEST)
        gathered = lax.all_to_all(
            lax.all_to_all(along_z, "row", split_axis=2, concat_axis=1, tiled=True),
            "col",
            split_axis=0,
            concat_axis=1,
            tiled=True,
        )
        piece_cells = gathered.shape[1] // (row_count * col_count)
        reordered = gathered.reshape(planes, col_count, row_count, piece_cells, rows_here)
        restored = jnp.transpose(reordered, (0, 4, 2, 1, 3)).reshape(planes, rows_here, line_length)
        update = STEP * line_solve(restored.reshape(-1, line_length), line_inverses).reshape(
            restored.shape
        )
        clamped = jnp.minimum(jnp.maximum(damage + update, lower_bound), 1.0)
        renewed = jnp.where(seeded, 1.0, clamped)
        own_sum = jnp.sum((renewed - damage) ** 2)
        own_sums.append(own_sum)
        damage = renewed
    global_sums = lax.psum(jnp.stack(own_sums), ("row", "col"))
    update_norms = jnp.sqrt(global_sums / cell_count + EPSILON) / STEP
    return (damage, update_norms)


def solution(mesh):
    return jax.shard_map(
        local,
        mesh=mesh,
        in_specs=(
            P("col", "row", None),
            P("col", "row", None),
            P("col", "row", None),
            P("col", "row", None),
            P(),
            P(),
        ),
        out_specs=(P("col", "row", None), P()),
        check_vma=False,
    )
```

profile of v0, /device:TPU:10, one launch (start us, length us, event | category | flops | bytes accessed | tf_op | source)
XLA Modules:
  0.0 739.1 jit_solution(10383993715968311955)
XLA Ops:
  5.4 6.2 copy.149
  11.6 6.4 broadcast_select_fusion.1
  32.9 7.5 %add_bitcast_fusion.1 = f32[1,2048,256]{2,0,1:T(1,128)} fusion(f32[1,256,2047]{1,0,2:T(1,128)S(1)} %slice_subtract_fusion.3, f32[1,256,2048]{1,0,2:T(1,128)S(1)} %copy.151, f32[1,256,2048]{1,0,2:T(1,128)} %broadcast_select_fusion.1), kind=kLoop, calls=%fused_computation.27 | loop fusion | flops 3145728 | bytes 8387584 | tf_op jit(solution)/shard_map/transpose | solution.py:70
  40.4 28.5 %all-to-all-done.2 = f32[1,2048,256]{2,0,1:T(1,128)} async-done(((f32[1,2048,256]{2,0,1:T(1,128)}), f32[1,2048,256]{2,0,1:T(1,128)}, u32[]{:S(2)}, u32[]{:S(2)}) %all-to-all-start.2) | async-done | bytes 2097184 | tf_op jit(solution)/shard_map/all_to_all | solution.py:82
  68.9 7.8 %all-to-all-start = ((f32[1,2048,256]{2,0,1:T(1,128)}), f32[1,2048,256]{2,0,1:T(1,128)}, u32[]{:S(2)}, u32[]{:S(2)}) async-start(f32[1,2048,256]{2,0,1:T(1,128)} %add_bitcast_fusion.1), calls=%async_computation | async-start | bytes 4194304 | tf_op jit(solution)/shard_map/all_to_all | solution.py:69
  80.2 6.1 copy.155
  86.3 35.9 %all-to-all-done = f32[1,2048,256]{2,0,1:T(1,128)} async-done(((f32[1,2048,256]{2,0,1:T(1,128)}), f32[1,2048,256]{2,0,1:T(1,128)}, u32[]{:S(2)}, u32[]{:S(2)}) %all-to-all-start) | async-done | bytes 2097184 | tf_op jit(solution)/shard_map/all_to_all | solution.py:69
  168.6 13.0 %all-to-all-done.1 = f32[1,256,2048]{2,0,1:T(1,128)} async-done(((f32[1,256,2048]{2,0,1:T(1,128)}), f32[1,256,2048]{2,0,1:T(1,128)}, u32[]{:S(2)}, u32[]{:S(2)}) %all-to-all-start.1) | async-done | bytes 2097184 | tf_op jit(solution)/shard_map/all_to_all | solution.py:68
  205.7 6.8 convolution_bitcast_fusion.1
  217.2 7.9 %reshape.1081 = f32[8,1,65536]{2,1,0:T(1,128)} reshape(f32[2048,4,64]{2,1,0:T(4,128)} %bitcast.194) | data formatting | bytes 4194304
  225.1 54.2 %all_to_all.174 = f32[8,1,65536]{2,1,0:T(1,128)} all-to-all(f32[8,1,65536]{2,1,0:T(1,128)} %reshape.1081), channel_id=1, replica_groups=mesh['row'=8,'col'=4] {'row'}, dimensions={0} | all-to-all | bytes 4194304 | tf_op jit(solution)/shard_map/all_to_all | solution.py:99
  279.8 8.6 %reduce = f32[8,65536]{1,0:T(8,128)} reduce(f32[8,1,65536]{2,1,0:T(1,128)} %all_to_all.174, f32[]{:T(128)} %broadcast.872), dimensions={1}, to_apply=%all_to_all.140.reduce_sub_computation | reduce | bytes 4194308 | tf_op jit(solution)/shard_map/all_to_all | solution.py:99
  288.4 6.4 reshape.1082
  311.8 17.4 %all-to-all-done.5 = f32[4,512,256]{2,1,0:T(8,128)} async-done(((f32[4,512,256]{2,1,0:T(8,128)}), f32[4,512,256]{2,1,0:T(8,128)}, u32[]{:S(2)}, u32[]{:S(2)}) %all-to-all-start.5) | async-done | bytes 2097184 | tf_op jit(solution)/shard_map/all_to_all | solution.py:98
  339.6 13.5 %minimum_select_fusion.1 = f32[1,256,2048]{1,0,2:T(1,128)} fusion(f32[1,256,2048]{1,0,2:T(1,128)} %broadcast_select_fusion.1, f32[1,256,2048]{1,2,0:T(8,128)S(1)} %bitcast.215, s32[1,256,2048]{1,0,2:T(1,128)S(1)} %copy-done.3, pred[1,256,2048]{1,0,2:T(4,128)(4,1)} %copy.170, f32[1,256,2048]{1,0,2:T(1,128)S(1)} %copy-done.5), kind=kLoop, calls=%fused_computation.21 | loop fusion | flops 3145728 | bytes 11010048 | tf_op jit(solution)/shard_map/jit(_where)/select_n | solution.py:112
  353.1 6.6 all-to-all-start.8
  364.0 6.6 add_bitcast_fusion
  370.6 34.7 %all-to-all-done.8 = f32[1,2048,256]{2,0,1:T(1,128)} async-done(((f32[1,2048,256]{2,0,1:T(1,128)}), f32[1,2048,256]{2,0,1:T(1,128)}, u32[]{:S(2)}, u32[]{:S(2)}) %all-to-all-start.8) | async-done | bytes 2097184 | tf_op jit(solution)/shard_map/all_to_all | solution.py:82
  405.3 7.8 %all-to-all-start.6 = ((f32[1,2048,256]{2,0,1:T(1,128)}), f32[1,2048,256]{2,0,1:T(1,128)}, u32[]{:S(2)}, u32[]{:S(2)}) async-start(f32[1,2048,256]{2,0,1:T(1,128)} %add_bitcast_fusion), calls=%async_computation.6 | async-start | bytes 4194304 | tf_op jit(solution)/shard_map/all_to_all | solution.py:69
  419.1 6.1 copy.176
  425.2 33.5 %all-to-all-done.6 = f32[1,2048,256]{2,0,1:T(1,128)} async-done(((f32[1,2048,256]{2,0,1:T(1,128)}), f32[1,2048,256]{2,0,1:T(1,128)}, u32[]{:S(2)}, u32[]{:S(2)}) %all-to-all-start.6) | async-done | bytes 2097184 | tf_op jit(solution)/shard_map/all_to_all | solution.py:69
  469.6 6.1 copy.174
  475.7 12.8 %all-to-all-done.9 = f32[1,256,2048]{2,0,1:T(1,128)} async-done(((f32[1,256,2048]{2,0,1:T(1,128)}), f32[1,256,2048]{2,0,1:T(1,128)}, u32[]{:S(2)}, u32[]{:S(2)}) %all-to-all-start.9) | async-done | bytes 2097184 | tf_op jit(solution)/shard_map/all_to_all | solution.py:81
  504.8 13.0 %all-to-all-done.7 = f32[1,256,2048]{2,0,1:T(1,128)} async-done(((f32[1,256,2048]{2,0,1:T(1,128)}), f32[1,256,2048]{2,0,1:T(1,128)}, u32[]{:S(2)}, u32[]{:S(2)}) %all-to-all-start.7) | async-done | bytes 2097184 | tf_op jit(solution)/shard_map/all_to_all | solution.py:68
  541.9 6.8 convolution_bitcast_fusion
  553.4 7.9 %reshape.1083 = f32[8,1,65536]{2,1,0:T(1,128)} reshape(f32[2048,4,64]{2,1,0:T(4,128)} %bitcast.196) | data formatting | bytes 4194304
  561.3 54.3 %all_to_all.175 = f32[8,1,65536]{2,1,0:T(1,128)} all-to-all(f32[8,1,65536]{2,1,0:T(1,128)} %reshape.1083), channel_id=1, replica_groups=mesh['row'=8,'col'=4] {'row'}, dimensions={0} | all-to-all | bytes 4194304 | tf_op jit(solution)/shard_map/all_to_all | solution.py:99
  615.6 8.5 %reduce.1 = f32[8,65536]{1,0:T(8,128)} reduce(f32[8,1,65536]{2,1,0:T(1,128)} %all_to_all.175, f32[]{:T(128)} %broadcast.872), dimensions={1}, to_apply=%all_to_all.157.reduce_sub_computation | reduce | bytes 4194308 | tf_op jit(solution)/shard_map/all_to_all | solution.py:99
  624.1 6.4 reshape.1084
  635.3 28.6 %all_to_all.176 = f32[4,512,256]{2,1,0:T(8,128)S(1)} all-to-all(f32[4,512,256]{2,1,0:T(8,128)} %bitcast.202), channel_id=1, replica_groups=mesh['row'=8,'col'=4] {'col'}, dimensions={0} | all-to-all | bytes 4194304 | tf_op jit(solution)/shard_map/all_to_all | solution.py:98
  672.6 16.7 %multiply_reduce_fusion.1 = (f32[]{:T(128)}, f32[]{:T(128)}, f32[1,256,2048]{1,0,2:T(1,128)}) fusion(f32[1,256,2048]{1,0,2:T(1,128)} %minimum_select_fusion.1, f32[1,256,2048]{1,0,2:T(1,128)} %broadcast_select_fusion.1, pred[1,256,2048]{1,0,2:T(4,128)(4,1)} %copy.170, f32[1,256,2048]{1,0,2:T(1,128)S(1)} %copy-done.6, f32[1,256,2048]{1,2,0:T(8,128)S(1)} %bitcast.218, ...), kind=kLoop, calls=%fused_computation.13 | loop fusion | flops 6291454 | bytes 13107208 | tf_op jit(solution)/shard_map/reduce_sum | solution.py:113
  690.7 41.4 %psum.7 = f32[2]{0:T(128)S(1)} all-reduce(f32[2]{0:T(128)S(1)} %pad_maximum_fusion), channel_id=1, replica_groups=mesh['row'=8,'col'=4] {'row','col'}, use_global_device_ids=true, to_apply=%region_2.3 | all-reduce | flops 2 | bytes 16 | tf_op jit(solution)/shard_map/psum | solution.py:116
  (137 shorter events, 205.6 us)
Async XLA Ops:
  0.6 205.0 %copy-start = (f32[4,4]{1,0:T(4,128)S(1)}, f32[4,4]{1,0:T(4,128)}, u32[]{:S(2)}) copy-start(f32[4,4]{1,0:T(4,128)} %param.11) | copy-start | bytes 196
  5.3 6.2 copy-start.2
  17.9 50.9 %all-to-all-start.2 = ((f32[1,2048,256]{2,0,1:T(1,128)}), f32[1,2048,256]{2,0,1:T(1,128)}, u32[]{:S(2)}, u32[]{:S(2)}) async-start(f32[1,2048,256]{2,0,1:T(1,128)} %bitcast.3), calls=%async_computation.2 | async-start | bytes 4194304 | tf_op jit(solution)/shard_map/all_to_all | solution.py:82
  28.0 4.9 copy-start.11
  68.9 53.4 %all-to-all-start = ((f32[1,2048,256]{2,0,1:T(1,128)}), f32[1,2048,256]{2,0,1:T(1,128)}, u32[]{:S(2)}, u32[]{:S(2)}) async-start(f32[1,2048,256]{2,0,1:T(1,128)} %add_bitcast_fusion.1), calls=%async_computation | async-start | bytes 4194304 | tf_op jit(solution)/shard_map/all_to_all | solution.py:69
  86.3 40.8 %copy-start.1 = (f32[8,256,256]{2,1,0:T(8,128)S(1)}, f32[8,256,256]{2,1,0:T(8,128)}, u32[]{:S(2)}) copy-start(f32[8,256,256]{2,1,0:T(8,128)} %param.10) | copy-start | bytes 6291460
  122.2 29.8 %all-to-all-start.3 = ((f32[1,256,2048]{2,0,1:T(1,128)}), f32[1,256,2048]{2,0,1:T(1,128)}, u32[]{:S(2)}, u32[]{:S(2)}) async-start(f32[1,256,2048]{2,0,1:T(1,128)} %copy.155), calls=%async_computation.3 | async-start | bytes 4194304 | tf_op jit(solution)/shard_map/all_to_all | solution.py:81
  152.0 29.6 %all-to-all-start.1 = ((f32[1,256,2048]{2,0,1:T(1,128)}), f32[1,256,2048]{2,0,1:T(1,128)}, u32[]{:S(2)}, u32[]{:S(2)}) async-start(f32[1,256,2048]{2,0,1:T(1,128)} %copy.153), calls=%async_computation.1 | async-start | bytes 4194304 | tf_op jit(solution)/shard_map/all_to_all | solution.py:68
  181.6 2.6 copy-start.13
  181.6 2.7 copy-start.15
  189.1 1.4 copy-start.8
  299.6 29.6 %all-to-all-start.5 = ((f32[4,512,256]{2,1,0:T(8,128)}), f32[4,512,256]{2,1,0:T(8,128)}, u32[]{:S(2)}, u32[]{:S(2)}) async-start(f32[4,512,256]{2,1,0:T(8,128)} %bitcast.198), calls=%async_computation.5 | async-start | bytes 4194304 | tf_op jit(solution)/shard_map/all_to_all | solution.py:98
  333.3 1.4 copy-start.9
  336.8 2.2 copy-start.3
  336.8 2.8 copy-start.5
  353.1 52.2 %all-to-all-start.8 = ((f32[1,2048,256]{2,0,1:T(1,128)}), f32[1,2048,256]{2,0,1:T(1,128)}, u32[]{:S(2)}, u32[]{:S(2)}) async-start(f32[1,2048,256]{2,0,1:T(1,128)} %bitcast.65), calls=%async_computation.8 | async-start | bytes 4194304 | tf_op jit(solution)/shard_map/all_to_all | solution.py:82
  359.7 4.3 copy-start.12
  405.3 53.4 %all-to-all-start.6 = ((f32[1,2048,256]{2,0,1:T(1,128)}), f32[1,2048,256]{2,0,1:T(1,128)}, u32[]{:S(2)}, u32[]{:S(2)}) async-start(f32[1,2048,256]{2,0,1:T(1,128)} %add_bitcast_fusion), calls=%async_computation.6 | async-start | bytes 4194304 | tf_op jit(solution)/shard_map/all_to_all | solution.py:69
  458.7 29.9 %all-to-all-start.9 = ((f32[1,256,2048]{2,0,1:T(1,128)}), f32[1,256,2048]{2,0,1:T(1,128)}, u32[]{:S(2)}, u32[]{:S(2)}) async-start(f32[1,256,2048]{2,0,1:T(1,128)} %copy.176), calls=%async_computation.9 | async-start | bytes 4194304 | tf_op jit(solution)/shard_map/all_to_all | solution.py:81
  488.6 29.2 %all-to-all-start.7 = ((f32[1,256,2048]{2,0,1:T(1,128)}), f32[1,256,2048]{2,0,1:T(1,128)}, u32[]{:S(2)}, u32[]{:S(2)}) async-start(f32[1,256,2048]{2,0,1:T(1,128)} %copy.174), calls=%async_computation.7 | async-start | bytes 4194304 | tf_op jit(solution)/shard_map/all_to_all | solution.py:68
  517.8 2.6 copy-start.14
  517.8 2.7 copy-start.16
  525.3 1.4 copy-start.10
  666.3 1.4 copy-start.7
  669.8 2.2 copy-start.4
  669.8 2.8 copy-start.6
where the time goes:
time: 748 us; the launch traced here: 739 us
  waiting for transfers between devices  190 us (25%)
  blocking collectives  178 us (24%)
  local copies, waits for them, and re-layouts  174 us (23%)
  other arithmetic  110 us (15%)
  starting transfers between devices  53.5 us (7%)
  matrix products  24 us (3%)
  between operations  9.76 us (1%)
    all_to_all x2, blocking collectives, local(): lax.all_to_all(along_z, 'row', split_axis=2, concat_axis=1, tiled=True)  108 us
    unnamed x54, local copies, waits for them, and re-layouts  81.7 us
    all_to_all x2, waiting for transfers between devices, local(): lax.all_to_all(jnp.swapaxes(partial_value, 1, 2), 'row', split_axis=1, co...  69.4 us
    all_to_all x2, waiting for transfers between devices, local(): lax.all_to_all(jnp.swapaxes(damage, 1, 2), 'row', split_axis=1, concat_ax...  63.1 us
    psum x1, blocking collectives, local(): global_sums = lax.psum(jnp.stack(own_sums), ('row', 'col'))  41.4 us
    all_to_all x1, blocking collectives, local(): lax.all_to_all(lax.all_to_all(along_z, 'row', split_axis=2, concat_axis=1...  28.6 us
    all_to_all x2, waiting for transfers between devices, local(): lax.all_to_all(lax.all_to_all(jnp.swapaxes(partial_value, 1, 2), 'row', s...  26 us
    another operation x4, local copies, waits for them, and re-layouts, local(): line_solve(turned.reshape(-1, turned_shape[2]), line_inverses)  20.3 us
  transfers between devices with their start and end apart: 9, of which 9 were waited for; matrix products, arithmetic and copies ran while one was open for 14% of the time, Pallas kernels for 0%

commit v1 on v0

--- a/solution.py
+++ b/solution.py
@@ -8,6 +8,12 @@
 STEP = 0.02
 COUPLE = 0.5
 EPSILON = 1e-06
+
+
+def trade_parts(value, axis, split, join):
+    pieces = jnp.split(value, lax.axis_size(axis), axis=split)
+    received = lax.all_to_all(jnp.stack(pieces), axis, 0, 0)
+    return jnp.concatenate(received, axis=join)
 
 
 def second_difference(grid_field, along):
@@ -79,9 +85,7 @@
                 tiled=True,
             ),
             lax.all_to_all(
-                lax.all_to_all(
-                    jnp.swapaxes(damage, 1, 2), "row", split_axis=1, concat_axis=2, tiled=True
-                ),
+                trade_parts(jnp.swapaxes(damage, 1, 2), "row", 1, 2),
                 "col",
                 split_axis=1,
                 concat_axis=0,

time: 748 us -> 775 us (1.036)
  local copies, waits for them, and re-layouts: 174 us -> 193 us
  waiting for transfers between devices: 190 us -> 203 us
  other arithmetic: 110 us -> 102 us
    another operation x0 -> x6, local copies, waits for them, and re-layouts: none -> 22.8 us  [trade_parts(): received = lax.all_to_all(jnp.stack(pieces), axis, 0, 0)]
    all_to_all x4 -> x0, local copies, waits for them, and re-layouts: 17 us -> none  [local(): lax.all_to_all(jnp.swapaxes(damage, 1, 2), 'row', split_axis=1, concat_ax...]
    reshape x0 -> x2, local copies, waits for them, and re-layouts: none -> 12.3 us  [trade_parts(): return jnp.concatenate(received, axis=join)]
    all_to_all x2, waiting for transfers between devices: 69.4 us -> 78.9 us  [local(): lax.all_to_all(jnp.swapaxes(partial_value, 1, 2), 'row', split_axis=1, co...]
    unnamed x54 -> x62, local copies, waits for them, and re-layouts: 81.7 us -> 80.4 us
  transfers between devices with their start and end apart: 9 -> 9, of which waited for: 9 -> 8; matrix products, arithmetic and copies ran while one was open for 14% -> 13% of each run, Pallas kernels for 0% -> 0%
where the time goes in v1:
time: 775 us; the launch traced here: 764 us
  waiting for transfers between devices  203 us (26%)
  local copies, waits for them, and re-layouts  193 us (25%)
  blocking collectives  178 us (23%)
  other arithmetic  102 us (13%)
  starting transfers between devices  53.1 us (7%)
  matrix products  24 us (3%)
  between operations  9.94 us (1%)
    all_to_all x2, blocking collectives, local(): lax.all_to_all(along_z, 'row', split_axis=2, concat_axis=1, tiled=True)  108 us
    unnamed x62, local copies, waits for them, and re-layouts  80.4 us
    all_to_all x2, waiting for transfers between devices, local(): lax.all_to_all(jnp.swapaxes(partial_value, 1, 2), 'row', split_axis=1, co...  78.9 us
    all_to_all x2, waiting for transfers between devices, trade_parts(): received = lax.all_to_all(jnp.stack(pieces), axis, 0, 0)  67.4 us
    psum x1, blocking collectives, local(): global_sums = lax.psum(jnp.stack(own_sums), ('row', 'col'))  41.4 us
    all_to_all x1, blocking collectives, local(): lax.all_to_all(lax.all_to_all(along_z, 'row', split_axis=2, concat_axis=1...  28.6 us
    all_to_all x2, waiting for transfers between devices, local(): lax.all_to_all(lax.all_to_all(jnp.swapaxes(partial_value, 1, 2), 'row', s...  26.8 us
    another operation x6, local copies, waits for them, and re-layouts, trade_parts(): received = lax.all_to_all(jnp.stack(pieces), axis, 0, 0)  22.8 us
  transfers between devices with their start and end apart: 9, of which 8 were waited for; matrix products, arithmetic and copies ran while one was open for 13% of the time, Pallas kernels for 0%

profile of v1, /device:TPU:10, one launch (start us, length us, event | category | flops | bytes accessed | tf_op | source)
XLA Modules:
  0.0 763.7 jit_solution(15732183006691959410)
XLA Ops:
  0.7 6.2 copy.204
  17.7 6.2 stack.261
  46.0 31.8 %all-to-all-done.2 = f32[8,1,256,256]{2,3,1,0:T(8,128)} async-done(((f32[8,1,256,256]{2,3,1,0:T(8,128)}), f32[8,1,256,256]{2,3,1,0:T(8,128)}, u32[]{:S(2)}, u32[]{:S(2)}) %all-to-all-start.2) | async-done | bytes 2097184 | tf_op jit(solution)/shard_map/all_to_all | solution.py:15
  77.8 7.8 %all-to-all-start = ((f32[1,2048,256]{2,0,1:T(1,128)}), f32[1,2048,256]{2,0,1:T(1,128)}, u32[]{:S(2)}, u32[]{:S(2)}) async-start(f32[1,2048,256]{2,0,1:T(1,128)} %add_bitcast_fusion.1), calls=%async_computation | async-start | bytes 4194304 | tf_op jit(solution)/shard_map/all_to_all | solution.py:75
  85.6 6.1 copy.212
  91.7 39.5 %all-to-all-done = f32[1,2048,256]{2,0,1:T(1,128)} async-done(((f32[1,2048,256]{2,0,1:T(1,128)}), f32[1,2048,256]{2,0,1:T(1,128)}, u32[]{:S(2)}, u32[]{:S(2)}) %all-to-all-start) | async-done | bytes 2097184 | tf_op jit(solution)/shard_map/all_to_all | solution.py:75
  156.7 6.1 copy.209
  178.9 13.8 %all-to-all-done.1 = f32[1,256,2048]{2,0,1:T(1,128)} async-done(((f32[1,256,2048]{2,0,1:T(1,128)}), f32[1,256,2048]{2,0,1:T(1,128)}, u32[]{:S(2)}, u32[]{:S(2)}) %all-to-all-start.1) | async-done | bytes 2097184 | tf_op jit(solution)/shard_map/all_to_all | solution.py:74
  217.4 6.9 convolution_bitcast_fusion.1
  229.0 7.9 %reshape.1097 = f32[8,1,65536]{2,1,0:T(1,128)} reshape(f32[2048,4,64]{2,1,0:T(4,128)} %bitcast.230) | data formatting | bytes 4194304
  236.9 54.1 %all_to_all.148 = f32[8,1,65536]{2,1,0:T(1,128)} all-to-all(f32[8,1,65536]{2,1,0:T(1,128)} %reshape.1097), channel_id=1, replica_groups=mesh['row'=8,'col'=4] {'row'}, dimensions={0} | all-to-all | bytes 4194304 | tf_op jit(solution)/shard_map/all_to_all | solution.py:103
  291.6 8.6 %reduce = f32[8,65536]{1,0:T(8,128)} reduce(f32[8,1,65536]{2,1,0:T(1,128)} %all_to_all.148, f32[]{:T(128)} %broadcast.872), dimensions={1}, to_apply=%all_to_all.117.reduce_sub_computation | reduce | bytes 4194308 | tf_op jit(solution)/shard_map/all_to_all | solution.py:103
  300.2 6.4 reshape.1098
  323.7 17.3 %all-to-all-done.5 = f32[4,512,256]{2,1,0:T(8,128)} async-done(((f32[4,512,256]{2,1,0:T(8,128)}), f32[4,512,256]{2,1,0:T(8,128)}, u32[]{:S(2)}, u32[]{:S(2)}) %all-to-all-start.5) | async-done | bytes 2097184 | tf_op jit(solution)/shard_map/all_to_all | solution.py:102
  351.8 12.5 %minimum_select_fusion.1 = f32[1,256,2048]{1,0,2:T(1,128)S(1)} fusion(f32[1,256,2048]{1,0,2:T(1,128)S(1)} %broadcast_select_fusion.1, f32[1,256,2048]{1,2,0:T(8,128)S(1)} %bitcast.247, s32[1,256,2048]{1,0,2:T(1,128)S(1)} %copy-done.8, pred[1,256,2048]{1,0,2:T(4,128)(4,1)} %copy.227, f32[1,256,2048]{1,0,2:T(1,128)S(1)} %copy-done.10), kind=kLoop, calls=%fused_computation.21 | loop fusion | flops 3145728 | bytes 11010048 | tf_op jit(solution)/shard_map/jit(_where)/select_n | solution.py:116
  366.6 6.2 stack.303
  375.8 6.6 all-to-all-start.8
  392.3 35.6 %all-to-all-done.8 = f32[8,1,256,256]{2,3,1,0:T(8,128)} async-done(((f32[8,1,256,256]{2,3,1,0:T(8,128)}), f32[8,1,256,256]{2,3,1,0:T(8,128)}, u32[]{:S(2)}, u32[]{:S(2)}) %all-to-all-start.8) | async-done | bytes 2097184 | tf_op jit(solution)/shard_map/all_to_all | solution.py:15
  427.9 7.8 %all-to-all-start.6 = ((f32[1,2048,256]{2,0,1:T(1,128)}), f32[1,2048,256]{2,0,1:T(1,128)}, u32[]{:S(2)}, u32[]{:S(2)}) async-start(f32[1,2048,256]{2,0,1:T(1,128)} %add_bitcast_fusion), calls=%async_computation.6 | async-start | bytes 4194304 | tf_op jit(solution)/shard_map/all_to_all | solution.py:75
  435.8 6.1 copy.234
  441.9 39.4 %all-to-all-done.6 = f32[1,2048,256]{2,0,1:T(1,128)} async-done(((f32[1,2048,256]{2,0,1:T(1,128)}), f32[1,2048,256]{2,0,1:T(1,128)}, u32[]{:S(2)}, u32[]{:S(2)}) %all-to-all-start.6) | async-done | bytes 2097184 | tf_op jit(solution)/shard_map/all_to_all | solution.py:75
  492.3 6.1 copy.231
  498.4 12.8 %all-to-all-done.9 = f32[1,256,2048]{2,0,1:T(1,128)} async-done(((f32[1,256,2048]{2,0,1:T(1,128)}), f32[1,256,2048]{2,0,1:T(1,128)}, u32[]{:S(2)}, u32[]{:S(2)}) %all-to-all-start.9) | async-done | bytes 2097184 | tf_op jit(solution)/shard_map/all_to_all | solution.py:87
  527.4 13.0 %all-to-all-done.7 = f32[1,256,2048]{2,0,1:T(1,128)} async-done(((f32[1,256,2048]{2,0,1:T(1,128)}), f32[1,256,2048]{2,0,1:T(1,128)}, u32[]{:S(2)}, u32[]{:S(2)}) %all-to-all-start.7) | async-done | bytes 2097184 | tf_op jit(solution)/shard_map/all_to_all | solution.py:74
  565.3 6.8 convolution_bitcast_fusion
  576.9 7.9 %reshape.1099 = f32[8,1,65536]{2,1,0:T(1,128)} reshape(f32[2048,4,64]{2,1,0:T(4,128)} %bitcast.232) | data formatting | bytes 4194304
  584.7 54.3 %all_to_all.149 = f32[8,1,65536]{2,1,0:T(1,128)} all-to-all(f32[8,1,65536]{2,1,0:T(1,128)} %reshape.1099), channel_id=1, replica_groups=mesh['row'=8,'col'=4] {'row'}, dimensions={0} | all-to-all | bytes 4194304 | tf_op jit(solution)/shard_map/all_to_all | solution.py:103
  639.0 8.6 %reduce.1 = f32[8,65536]{1,0:T(8,128)} reduce(f32[8,1,65536]{2,1,0:T(1,128)} %all_to_all.149, f32[]{:T(128)} %broadcast.872), dimensions={1}, to_apply=%all_to_all.131.reduce_sub_computation | reduce | bytes 4194308 | tf_op jit(solution)/shard_map/all_to_all | solution.py:103
  647.6 6.4 reshape.1100
  658.8 28.6 %all_to_all.150 = f32[4,512,256]{2,1,0:T(8,128)S(1)} all-to-all(f32[4,512,256]{2,1,0:T(8,128)} %bitcast.238), channel_id=1, replica_groups=mesh['row'=8,'col'=4] {'col'}, dimensions={0} | all-to-all | bytes 4194304 | tf_op jit(solution)/shard_map/all_to_all | solution.py:102
  697.6 16.4 %multiply_reduce_fusion.1 = (f32[]{:T(128)}, f32[]{:T(128)}, f32[1,256,2048]{1,0,2:T(1,128)}) fusion(f32[1,256,2048]{1,0,2:T(1,128)S(1)} %copy-done.3, f32[1,256,2048]{1,0,2:T(1,128)S(1)} %broadcast_select_fusion.1, pred[1,256,2048]{1,0,2:T(4,128)(4,1)} %copy.227, f32[1,256,2048]{1,0,2:T(1,128)} %copy.205, f32[1,256,2048]{1,2,0:T(8,128)S(1)} %bitcast.250, ...), kind=kLoop, calls=%fused_computation.13 | loop fusion | flops 6291454 | bytes 13107208 | tf_op jit(solution)/shard_map/reduce_sum | solution.py:117
  715.3 41.4 %psum.7 = f32[2]{0:T(128)S(1)} all-reduce(f32[2]{0:T(128)S(1)} %pad_maximum_fusion), channel_id=1, replica_groups=mesh['row'=8,'col'=4] {'row','col'}, use_global_device_ids=true, to_apply=%region_2.3 | all-reduce | flops 2 | bytes 16 | tf_op jit(solution)/shard_map/psum | solution.py:120
  (149 shorter events, 218.5 us)
Async XLA Ops:
  0.6 216.8 %copy-start = (f32[4,4]{1,0:T(4,128)S(1)}, f32[4,4]{1,0:T(4,128)}, u32[]{:S(2)}) copy-start(f32[4,4]{1,0:T(4,128)} %param.11) | copy-start | bytes 196
  0.6 6.2 copy-start.21
  26.8 50.9 %all-to-all-start.2 = ((f32[8,1,256,256]{2,3,1,0:T(8,128)}), f32[8,1,256,256]{2,3,1,0:T(8,128)}, u32[]{:S(2)}, u32[]{:S(2)}) async-start(f32[8,1,256,256]{2,3,1,0:T(8,128)} %copy.210), calls=%async_computation.2 | async-start | bytes 4194304 | tf_op jit(solution)/shard_map/all_to_all | solution.py:15
  38.2 2.2 copy-start.15
  77.8 53.4 %all-to-all-start = ((f32[1,2048,256]{2,0,1:T(1,128)}), f32[1,2048,256]{2,0,1:T(1,128)}, u32[]{:S(2)}, u32[]{:S(2)}) async-start(f32[1,2048,256]{2,0,1:T(1,128)} %add_bitcast_fusion.1), calls=%async_computation | async-start | bytes 4194304 | tf_op jit(solution)/shard_map/all_to_all | solution.py:75
  131.1 31.6 %all-to-all-start.3 = ((f32[1,256,2048]{2,0,1:T(1,128)}), f32[1,256,2048]{2,0,1:T(1,128)}, u32[]{:S(2)}, u32[]{:S(2)}) async-start(f32[1,256,2048]{2,0,1:T(1,128)} %copy.212), calls=%async_computation.3 | async-start | bytes 4194304 | tf_op jit(solution)/shard_map/all_to_all | solution.py:87
  162.8 29.9 %all-to-all-start.1 = ((f32[1,256,2048]{2,0,1:T(1,128)}), f32[1,256,2048]{2,0,1:T(1,128)}, u32[]{:S(2)}, u32[]{:S(2)}) async-start(f32[1,256,2048]{2,0,1:T(1,128)} %copy.209), calls=%async_computation.1 | async-start | bytes 4194304 | tf_op jit(solution)/shard_map/all_to_all | solution.py:74
  192.7 2.6 copy-start.17
  192.7 2.7 copy-start.19
  196.4 1.6 copy-start.4
  200.9 1.3 copy-start.12
  311.4 29.6 %all-to-all-start.5 = ((f32[4,512,256]{2,1,0:T(8,128)}), f32[4,512,256]{2,1,0:T(8,128)}, u32[]{:S(2)}, u32[]{:S(2)}) async-start(f32[4,512,256]{2,1,0:T(8,128)} %bitcast.234), calls=%async_computation.5 | async-start | bytes 4194304 | tf_op jit(solution)/shard_map/all_to_all | solution.py:102
  341.0 2.2 copy-start.5
  345.5 1.3 copy-start.13
  349.0 2.2 copy-start.8
  349.0 2.8 copy-start.10
  364.3 2.3 copy-start.1
  375.8 52.2 %all-to-all-start.8 = ((f32[8,1,256,256]{2,3,1,0:T(8,128)}), f32[8,1,256,256]{2,3,1,0:T(8,128)}, u32[]{:S(2)}, u32[]{:S(2)}) async-start(f32[8,1,256,256]{2,3,1,0:T(8,128)} %copy.232), calls=%async_computation.8 | async-start | bytes 4194304 | tf_op jit(solution)/shard_map/all_to_all | solution.py:15
  382.4 4.5 copy-start.2
  382.4 4.5 copy-start.16
  427.9 53.4 %all-to-all-start.6 = ((f32[1,2048,256]{2,0,1:T(1,128)}), f32[1,2048,256]{2,0,1:T(1,128)}, u32[]{:S(2)}, u32[]{:S(2)}) async-start(f32[1,2048,256]{2,0,1:T(1,128)} %add_bitcast_fusion), calls=%async_computation.6 | async-start | bytes 4194304 | tf_op jit(solution)/shard_map/all_to_all | solution.py:75
  481.4 29.9 %all-to-all-start.9 = ((f32[1,256,2048]{2,0,1:T(1,128)}), f32[1,256,2048]{2,0,1:T(1,128)}, u32[]{:S(2)}, u32[]{:S(2)}) async-start(f32[1,256,2048]{2,0,1:T(1,128)} %copy.234), calls=%async_computation.9 | async-start | bytes 4194304 | tf_op jit(solution)/shard_map/all_to_all | solution.py:87
  511.2 29.2 %all-to-all-start.7 = ((f32[1,256,2048]{2,0,1:T(1,128)}), f32[1,256,2048]{2,0,1:T(1,128)}, u32[]{:S(2)}, u32[]{:S(2)}) async-start(f32[1,256,2048]{2,0,1:T(1,128)} %copy.231), calls=%async_computation.7 | async-start | bytes 4194304 | tf_op jit(solution)/shard_map/all_to_all | solution.py:74
  540.4 2.6 copy-start.18
  540.4 2.7 copy-start.20
  544.2 1.6 copy-start.6
  548.7 1.3 copy-start.14
  687.4 1.6 copy-start.7
  691.3 1.4 copy-start.11
  694.8 2.2 copy-start.3
  694.8 2.8 copy-start.9
